TPU v7x, 32 devices: a whole 2x2x4 slice. The times are simulated.
32 devices in a mesh: row: 4 (over z), col: 8 (over y, x, core).
Axes of the slice: x: 2, y: 2, z: 4, core: 2. Of those that a mesh axis runs over, the one named last changes fastest.
Arguments:
- pencil_a: float32 [4, 3072, 8, 1536], P('row', None, 'col'), may hold values from -6 to 6, as said below
- pencil_b: float32 [4, 3072, 8, 1536], P('row', None, 'col'), may hold values from -6 to 6
Outputs:
- new_a: float32 [4, 3072, 8, 1536], P('row', None, 'col')
- new_b: float32 [4, 3072, 8, 1536], P('row', None, 'col')
Inputs may be any that keep to these rules, and one draw needn't show every extreme that they name: `pencil_a`: the first 256 columns of Amat are zero in the last 256 rows of Amat.
All inputs are finite; a program needn't handle non-finite values.
Results may differ from a plain program's by a relative error of at most 0.000056.
Values sent between devices are 32-bit elements; how exact they have to be, the bound alone decides.
A program may use at most 192 MiB of HBM per device.

v0:
```python
import jax
import jax.numpy as jnp
from jax import lax
from jax.sharding import PartitionSpec as P

NB = 256


def broadcast(array, axis, root):
    mine = lax.axis_index(axis) == root
    return lax.psum(jnp.where(mine, array, jnp.zeros_like(array)), axis)


def matmul(left, right):
    return jnp.dot(left, right, precision=lax.Precision.HIGHEST, preferred_element_type=jnp.float32)


def inverse_factor(gram):
    lower = jnp.linalg.cholesky(gram)
    ident = jnp.eye(gram.shape[0], dtype=jnp.float32)
    return jax.scipy.linalg.solve_triangular(lower, ident, lower=True).T


def general_inverse(square):
    lower = jnp.linalg.cholesky(matmul(square, square.T))
    ident = jnp.eye(square.shape[0], dtype=jnp.float32)
    linv = jax.scipy.linalg.solve_triangular(lower, ident, lower=True)
    return matmul(square.T, matmul(linv.T, linv))


def fast_matmul(left, right):
    return jnp.dot(left, right, precision=lax.Precision.HIGH, preferred_element_type=jnp.float32)


def on_device(pencil_a, pencil_b):
    rows_loc = pencil_a.shape[1]
    cols_loc = pencil_a.shape[3]
    amat = pencil_a.reshape(rows_loc, cols_loc)
    bmat = pencil_b.reshape(rows_loc, cols_loc)
    width = NB
    ident = jnp.eye(width, dtype=jnp.float32)
    row = lax.axis_index("row")
    col = lax.axis_index("col")
    last_row = lax.axis_size("row") - 1
    last_col = lax.axis_size("col") - 1
    top_mask = (row == 0).astype(jnp.float32)
    end_mask = (col == last_col).astype(jnp.float32)
    own_panel = amat[:, :width]
    own_strip = bmat[rows_loc - width :]
    zero = jnp.zeros((width, width), jnp.float32)
    small = jnp.stack(
        [
            jnp.where(col == 0, matmul(own_panel.T, own_panel), zero),
            jnp.where((col == 0) & (row == 0), own_panel[:width], zero),
            jnp.where(row == last_row, matmul(own_strip, own_strip.T), zero),
            jnp.where(
                (col == last_col) & (row == last_row), own_strip[:, cols_loc - width :], zero
            ),
        ]
    )
    small = lax.psum(small, ("row", "col"))
    own_panel, own_strip, small = lax.optimization_barrier((own_panel, own_strip, small))
    panel = broadcast(own_panel, "col", 0)
    strip = broadcast(own_strip, "row", last_row)
    left_inv = inverse_factor(small[0])
    right_inv = inverse_factor(small[2])
    vectors = matmul(panel, left_inv) + top_mask * jnp.pad(ident, ((0, rows_loc - width), (0, 0)))
    vectors_t = matmul(right_inv.T, strip) + end_mask * jnp.pad(
        ident, ((0, 0), (cols_loc - width, 0))
    )
    vectors, strip = lax.optimization_barrier((vectors, strip))
    products_a, products_b = lax.psum(
        (fast_matmul(vectors.T, amat), fast_matmul(vectors.T, bmat)), "row"
    )
    share = lax.psum_scatter(
        jnp.concatenate([fast_matmul(amat, vectors_t.T), fast_matmul(bmat, vectors_t.T)], axis=1),
        "col",
        scatter_dimension=0,
        tiled=True,
    )
    kinv_right = general_inverse(ident + matmul(right_inv.T, small[3]).T)
    kinv_left = general_inverse(ident + matmul(small[1], left_inv))
    scaled = jnp.concatenate(
        [matmul(share[:, :width], kinv_right.T), matmul(share[:, width:], kinv_right.T)], axis=1
    )
    gathered = lax.all_gather(scaled, "col", axis=0, tiled=True)
    cross = lax.psum(
        jnp.concatenate([matmul(products_a, vectors_t.T), matmul(products_b, vectors_t.T)], axis=0),
        "col",
    )

    def update(matrix, products, mixed, crossed):
        inner = products - matmul(matmul(crossed, kinv_right.T), vectors_t)
        low = jnp.concatenate([matmul(kinv_left, inner), vectors_t], axis=0)
        return matrix - fast_matmul(jnp.concatenate([vectors, mixed], axis=1), low)

    amat = update(amat, products_a, gathered[:, :width], cross[:width])
    bmat = update(bmat, products_b, gathered[:, width:], cross[width:])
    return (amat.reshape(1, rows_loc, 1, cols_loc), bmat.reshape(1, rows_loc, 1, cols_loc))


def solution(mesh):
    placed = (P("row", None, "col", None), P("row", None, "col", None))
    return jax.shard_map(
        on_device,
        mesh=mesh,
        in_specs=placed,
        out_specs=(P("row", None, "col", None), P("row", None, "col", None)),
        check_vma=False,
    )
```

profile of v0, /device:TPU:0, one launch (start us, length us, event | category | flops | bytes accessed | tf_op | source)
XLA Modules:
  0.0 798.0 jit_solution(4191456055535194326)
XLA Ops:
  12.6 39.6 %copy.4 = f32[1,3072,1,1536]{1,3,2,0:T(8,128)} copy(f32[1,3072,1,1536]{3,2,1,0:T(1,128)} %param.5) | data formatting | bytes 37748736 | tf_op args[0]
  63.9 129.5 %all-reduce.10.cloned.1.call-done = f32[4,256,256]{1,2,0:T(8,128)} async-done(((f32[4,256,256]{1,2,0:T(8,128)}), f32[4,256,256]{1,2,0:T(8,128)}) %all-reduce.10.cloned.1.call-update) | async-done | bytes 1048592 | tf_op jit(solution)/shard_map/psum | solution.py:61
  201.9 11.7 %cholesky.248 = f32[128,128]{1,0:T(8,128)S(1)} custom-call(f32[128,128]{1,0:T(8,128)S(1)} %cholesky.349), custom_call_target="Cholesky" | custom-call | tf_op jit(solution)/shard_map/jit(cholesky)/cholesky | solution.py:19
  249.6 11.7 %cholesky.265 = f32[128,128]{1,0:T(8,128)S(1)} custom-call(f32[128,128]{1,0:T(8,128)S(1)} %convolution_subtract_fusion.8), custom_call_target="Cholesky" | custom-call | tf_op jit(solution)/shard_map/jit(cholesky)/cholesky | solution.py:19
  264.2 11.7 %cholesky.231 = f32[128,128]{1,0:T(8,128)S(1)} custom-call(f32[128,128]{1,0:T(8,128)S(1)} %convolution_subtract_fusion.9), custom_call_target="Cholesky" | custom-call | tf_op jit(solution)/shard_map/jit(cholesky)/cholesky | solution.py:19
  288.8 19.7 %custom-call.20 = f32[2,128,128]{1,2,0:T(8,128)S(1)} custom-call(f32[2,128,128]{2,1,0:T(8,128)S(1)} %get-tuple-element.39), custom_call_target="InvertDiagBlocksLowerTriangular" | custom-call | tf_op jit(solution)/shard_map/jit(_solve_triangular)/triangular_solve | solution.py:21
  308.5 19.7 %custom-call.18 = f32[2,128,128]{1,2,0:T(8,128)S(1)} custom-call(f32[2,128,128]{2,1,0:T(8,128)S(1)} %get-tuple-element.38), custom_call_target="InvertDiagBlocksLowerTriangular" | custom-call | tf_op jit(solution)/shard_map/jit(_solve_triangular)/triangular_solve | solution.py:21
  337.7 14.5 %all-reduce.14.cloned.1.call-done = f32[256,1536]{0,1:T(8,128)} async-done(((f32[256,1536]{0,1:T(8,128)}), f32[256,1536]{0,1:T(8,128)}) %all-reduce.14.cloned.1.call-update) | async-done | bytes 1572880 | tf_op jit(solution)/shard_map/psum | solution.py:11
  352.2 17.5 %fusion = f32[256,1536]{1,0:T(8,128)} fusion(f32[3072,256]{1,0:T(8,128)S(1)} %convolution_add_fusion, f32[1,3072,1,1536]{3,2,1,0:T(1,128)} %param.6), kind=kOutput, calls=%fused_computation.9 | convolution fusion | flops 7247757312 | bytes 23592960 | tf_op jit(solution)/shard_map/dot_general | solution.py:32
  369.6 19.3 %fusion.80 = f32[256,1536]{1,0:T(8,128)} fusion(f32[3072,256]{1,0:T(8,128)S(1)} %convolution_add_fusion, f32[1,3072,1,1536]{1,3,2,0:T(8,128)} %copy.4), kind=kOutput, calls=%fused_computation.170 | convolution fusion | flops 7247757312 | bytes 23592960 | tf_op jit(solution)/shard_map/dot_general | solution.py:32
  394.2 15.4 %fusion.9 = f32[3072,256]{0,1:T(8,128)S(1)} fusion(f32[256,1536]{1,0:T(8,128)S(1)} %convolution_add_fusion.1, f32[1,3072,1,1536]{3,2,1,0:T(1,128)} %param.6), kind=kOutput, calls=%fused_computation.22 | convolution fusion | flops 7247757312 | bytes 23592960 | tf_op jit(solution)/shard_map/dot_general | solution.py:32
  409.6 11.9 %convolution_bitcast_fusion = f32[3072,256]{0,1:T(8,128)S(1)} fusion(f32[256,1536]{1,0:T(8,128)S(1)} %convolution_add_fusion.1, f32[1,3072,1,1536]{1,3,2,0:T(8,128)} %copy.4), kind=kOutput, calls=%fused_computation.23 | convolution fusion | flops 7247757312 | bytes 23592960 | tf_op jit(solution)/shard_map/dot_general | solution.py:32
  429.2 11.7 %cholesky.282 = f32[128,128]{1,0:T(8,128)S(1)} custom-call(f32[128,128]{1,0:T(8,128)S(1)} %cholesky.352), custom_call_target="Cholesky" | custom-call | tf_op jit(solution)/shard_map/jit(cholesky)/cholesky | solution.py:25
  455.6 13.2 %cholesky.299 = f32[128,128]{1,0:T(8,128)} custom-call(f32[128,128]{1,0:T(8,128)} %convolution_subtract_fusion.7), custom_call_target="Cholesky" | custom-call | tf_op jit(solution)/shard_map/jit(cholesky)/cholesky | solution.py:25
  479.3 21.1 %custom-call.22 = f32[2,128,128]{1,2,0:T(8,128)} custom-call(f32[2,128,128]{2,1,0:T(8,128)} %get-tuple-element.40), custom_call_target="InvertDiagBlocksLowerTriangular" | custom-call | tf_op jit(solution)/shard_map/jit(_solve_triangular)/triangular_solve | solution.py:27
  514.7 58.9 %reduce-scatter.2.cloned.1.call-done = f32[384,512]{0,1:T(8,128)} async-done(((f32[3072,512]{0,1:T(8,128)}), f32[384,512]{0,1:T(8,128)}) %reduce-scatter.2.cloned.1.call-update) | async-done | bytes 786448 | tf_op jit(solution)/shard_map/reduce_scatter | solution.py:75
  580.4 11.7 %cholesky.316 = f32[128,128]{1,0:T(8,128)S(1)} custom-call(f32[128,128]{1,0:T(8,128)S(1)} %cholesky.355), custom_call_target="Cholesky" | custom-call | tf_op jit(solution)/shard_map/jit(cholesky)/cholesky | solution.py:25
  602.4 12.1 %cholesky.333 = f32[128,128]{1,0:T(8,128)S(1)} custom-call(f32[128,128]{1,0:T(8,128)S(1)} %convolution_subtract_fusion.6), custom_call_target="Cholesky" | custom-call | tf_op jit(solution)/shard_map/jit(cholesky)/cholesky | solution.py:25
  620.9 19.7 %custom-call.24 = f32[2,128,128]{1,2,0:T(8,128)S(1)} custom-call(f32[2,128,128]{2,1,0:T(8,128)S(1)} %get-tuple-element.41), custom_call_target="InvertDiagBlocksLowerTriangular" | custom-call | tf_op jit(solution)/shard_map/jit(_solve_triangular)/triangular_solve | solution.py:27
  654.2 24.6 %all-gather.2.cloned.1.call-done = f32[3072,512]{1,0:T(8,128)} async-done(((f32[384,512]{1,0:T(8,128)}), f32[3072,512]{1,0:T(8,128)}) %all-gather.2.cloned.1.call-update) | async-done | bytes 6291472 | tf_op jit(solution)/shard_map/all_gather | solution.py:86
  683.9 20.7 %subtract_bitcast_fusion = f32[1,3072,1,1536]{1,3,2,0:T(8,128)} fusion(f32[3072,256]{1,0:T(8,128)S(1)} %copy-done.1, f32[3072,256]{1,0:T(8,128)S(1)} %get-tuple-element.87, f32[256,1536]{1,0:T(8,128)S(1)} %convolution_add_fusion.1, f32[256,1536]{1,0:T(8,128)S(1)} %copy-done.2, f32[1,3072,1,1536]{1,3,2,0:T(8,128)} %copy.4), kind=kOutput, calls=%fused_computation.14 | convolution fusion | flops 14502592512 | bytes 47185920 | tf_op jit(solution)/shard_map/dot_general | solution.py:32
  704.5 39.7 %copy.15 = f32[1,3072,1,1536]{3,2,1,0:T(1,128)} copy(f32[1,3072,1,1536]{1,3,2,0:T(8,128)} %subtract_bitcast_fusion) | data formatting | bytes 37748736
  744.2 24.4 %fusion.4 = f32[1,3072,1,1536]{3,1,2,0:T(8,128)} fusion(f32[1,3072,1,1536]{3,2,1,0:T(1,128)} %param.6, f32[3072,256]{1,0:T(8,128)} %copy-done, f32[3072,256]{1,0:T(8,128)} %get-tuple-element.86, f32[256,1536]{1,0:T(8,128)S(1)} %convolution_add_fusion.1, f32[256,1536]{1,0:T(8,128)S(1)} %fusion.96), kind=kOutput, calls=%fused_computation.13 | convolution fusion | flops 14502592512 | bytes 47185920 | tf_op jit(solution)/shard_map/dot_general | solution.py:32
  768.6 22.3 %copy.16 = f32[1,3072,1,1536]{3,2,1,0:T(1,128)} copy(f32[1,3072,1,1536]{3,1,2,0:T(8,128)} %fusion.4) | data formatting | bytes 37748736
  (183 shorter events, 192.6 us)
Async XLA Ops:
  7.2 1.4 slice-start
  7.2 186.2 %all-reduce.10.cloned.1.call-start = ((), (), s32[]{:S(2)}) async-start(), calls=%async_computation.1 | async-start | bytes 2097152 | tf_op jit(solution)/shard_map/psum | solution.py:61
  59.9 270.8 %all-reduce.12.cloned.1.call-start = ((), (), s32[]{:S(2)}) async-start(), calls=%async_computation.2 | async-start | bytes 6291456 | tf_op jit(solution)/shard_map/psum | solution.py:11
  197.3 1.2 copy-start.7
  197.3 154.9 %all-reduce.14.cloned.1.call-start = ((), (), s32[]{:S(2)}) async-start(), calls=%async_computation.3 | async-start | bytes 3145728 | tf_op jit(solution)/shard_map/psum | solution.py:11
  284.4 46.3 %copy-start.11 = (f32[256,256]{1,0:T(8,128)}, f32[256,256]{1,0:T(8,128)S(1)}, u32[]{:S(2)}) copy-start(f32[256,256]{1,0:T(8,128)S(1)} %get-tuple-element.325) | copy-start | bytes 786436
  284.5 224.7 %all-reduce.18.cloned.1.call-start = ((), (), s32[]{:S(2)}) async-start(), calls=%async_computation.7 | async-start | bytes 6291456 | tf_op jit(solution)/shard_map/psum | solution.py:72
  308.5 20.7 %copy-start.16 = (f32[2,128,128]{1,2,0:T(8,128)}, f32[2,128,128]{1,2,0:T(8,128)S(1)}, u32[]{:S(2)}) copy-start(f32[2,128,128]{1,2,0:T(8,128)S(1)} %custom-call.20) | copy-start | bytes 393220
  337.7 32.0 %copy-start = (f32[3072,256]{1,0:T(8,128)}, f32[3072,256]{1,0:T(8,128)S(1)}, u32[]{:S(2)}) copy-start(f32[3072,256]{1,0:T(8,128)S(1)} %convolution_add_fusion) | copy-start | bytes 9437188
  388.9 0.9 copy-start.10
  388.9 2.0 copy-start.17
  388.9 184.7 %reduce-scatter.2.cloned.1.call-start = ((), (), s32[]{:S(2)}) async-start(), calls=%async_computation.4 | async-start | bytes 7077888 | tf_op jit(solution)/shard_map/reduce_scatter | solution.py:75
  424.6 1.2 copy-start.8
  424.6 219.8 %all-reduce.16.cloned.1.call-start = ((), (), s32[]{:S(2)}) async-start(), calls=%async_computation.6 | async-start | bytes 1048576 | tf_op jit(solution)/shard_map/psum | solution.py:87
  428.5 0.7 copy-start.13
  470.4 1.9 copy-start.12
  509.1 3.0 copy-start.4
  514.5 164.3 %all-gather.2.cloned.1.call-start = ((), (), s32[]{:S(2)}) async-start(), calls=%async_computation.5 | async-start | bytes 7077888 | tf_op jit(solution)/shard_map/all_gather | solution.py:86
  579.7 61.2 %copy-start.6 = (f32[256,256]{1,0:T(8,128)}, f32[256,256]{1,0:T(8,128)S(1)}, u32[]{:S(2)}) copy-start(f32[256,256]{1,0:T(8,128)S(1)} %convolution_add_fusion.2) | copy-start | bytes 786436
  641.2 6.0 copy-start.5
  644.4 4.3 copy-start.9
  647.2 3.0 copy-start.3
  678.8 5.1 copy-start.1
  678.8 5.1 copy-start.2
  (2 other events, 1.3 us)
Sparse Core Ops, SparseCore 0:
  60.0 133.3 all-reduce.9
  197.4 68.5 all-reduce.11
  284.6 67.5 all-reduce.13
  389.1 120.0 all-reduce.17
  512.9 60.6 reduce-scatter.1
  576.6 55.6 all-reduce.15
  634.2 44.5 all-gather.1
where the time goes:
time: 807 us; the launch traced here: 798 us
  other arithmetic  237 us (29%)
  waiting for transfers between devices  233 us (29%)
  matrix products  167 us (21%)
  local copies, waits for them, and re-layouts  140 us (17%)
  between operations  19.9 us (2%)
    psum x1, waiting for transfers between devices, on_device(): small = lax.psum(small, ('row', 'col'))  130 us
    dot_general x6, matrix products, fast_matmul(): jnp.dot(left, right, precision=lax.Precision.HIGH, preferred_element_type...  109 us
    unnamed x40, local copies, waits for them, and re-layouts  108 us
    another operation x14, other arithmetic, general_inverse(): lower = jnp.linalg.cholesky(matmul(square, square.T))  72.6 us
    another operation x14, other arithmetic, inverse_factor(): lower = jnp.linalg.cholesky(gram)  69.4 us
    reduce_scatter x1, waiting for transfers between devices, on_device(): lax.psum_scatter(jnp.concatenate([fast_matmul(amat, vectors_t.T), fast_ma...  58.9 us
    dot_general x22, matrix products, matmul(): jnp.dot(left, right, precision=lax.Precision.HIGHEST, preferred_element_t...  42.6 us
    another operation x4, other arithmetic, general_inverse(): linv = jax.scipy.linalg.solve_triangular(lower, ident, lower=True)  41.8 us
  transfers between devices with their start and end apart: 7, of which 5 were waited for; matrix products, arithmetic and copies ran while one was open for 42% of the time, Pallas kernels for 0%

commit v1 on v0

--- a/solution.py
+++ b/solution.py
@@ -58,7 +58,7 @@
             ),
         ]
     )
-    small = lax.psum(small, ("row", "col"))
+    small = jnp.sum(lax.all_gather(small, ("row", "col")), axis=0)
     own_panel, own_strip, small = lax.optimization_barrier((own_panel, own_strip, small))
     panel = broadcast(own_panel, "col", 0)
     strip = broadcast(own_strip, "row", last_row)

time: 807 us -> 842 us (1.043)
  waiting for transfers between devices: 233 us -> 297 us
  local copies, waits for them, and re-layouts: 140 us -> 98 us
  other arithmetic: 237 us -> 248 us
    all_gather x0 -> x1, waiting for transfers between devices: none -> 195 us  [on_device(): small = jnp.sum(lax.all_gather(small, ('row', 'col')), axis=0)]
    psum x1 -> x0, waiting for transfers between devices: 130 us -> none  [on_device(): small = lax.psum(small, ('row', 'col'))]
    unnamed x40 -> x38, local copies, waits for them, and re-layouts: 108 us -> 65.7 us
    reduce_sum x0 -> x1, other arithmetic: none -> 12.9 us  [on_device(): small = jnp.sum(lax.all_gather(small, ('row', 'col')), axis=0)]
  transfers between devices with their start and end apart: 7 -> 7, of which waited for: 5 -> 5; matrix products, arithmetic and copies ran while one was open for 42% -> 40% of each run, Pallas kernels for 0% -> 0%
where the time goes in v1:
time: 842 us; the launch traced here: 833 us
  waiting for transfers between devices  297 us (35%)
  other arithmetic  248 us (29%)
  matrix products  168 us (20%)
  local copies, waits for them, and re-layouts  98 us (12%)
  between operations  19.9 us (2%)
    all_gather x1, waiting for transfers between devices, on_device(): small = jnp.sum(lax.all_gather(small, ('row', 'col')), axis=0)  195 us
    dot_general x6, matrix products, fast_matmul(): jnp.dot(left, right, precision=lax.Precision.HIGH, preferred_element_type...  112 us
    another operation x14, other arithmetic, general_inverse(): lower = jnp.linalg.cholesky(matmul(square, square.T))  72.6 us
    another operation x14, other arithmetic, inverse_factor(): lower = jnp.linalg.cholesky(gram)  69.4 us
    unnamed x38, local copies, waits for them, and re-layouts  65.7 us
    reduce_scatter x1, waiting for transfers between devices, on_device(): lax.psum_scatter(jnp.concatenate([fast_matmul(amat, vectors_t.T), fast_ma...  58.9 us
    another operation x4, other arithmetic, general_inverse(): linv = jax.scipy.linalg.solve_triangular(lower, ident, lower=True)  41.8 us
    dot_general x22, matrix products, matmul(): jnp.dot(left, right, precision=lax.Precision.HIGHEST, preferred_element_t...  41.4 us
  transfers between devices with their start and end apart: 7, of which 5 were waited for; matrix products, arithmetic and copies ran while one was open for 40% of the time, Pallas kernels for 0%

profile of v1, /device:TPU:0, one launch (start us, length us, event | category | flops | bytes accessed | tf_op | source)
XLA Modules:
  0.0 833.1 jit_solution(17811043873348135209)
XLA Ops:
  11.3 16.4 %copy.47 = f32[1,3072,1,1536]{3,1,2,0:T(8,128)} copy(f32[1,3072,1,1536]{3,2,1,0:T(1,128)} %param.5) | data formatting | bytes 37748736
  40.1 194.8 %all-gather.6.cloned.1.call-done = f32[128,256,256]{2,1,0:T(8,128)} async-done(((f32[4,256,256]{2,1,0:T(8,128)}), f32[128,256,256]{2,1,0:T(8,128)}) %all-gather.6.cloned.1.call-update) | async-done | bytes 33554448 | tf_op jit(solution)/shard_map/all_gather | solution.py:61
  234.9 12.9 %reduce_sum.9 = f32[4,256,256]{2,1,0:T(8,128)} reduce(f32[32,4,256,256]{3,2,1,0:T(8,128)} %bitcast.207, f32[]{:T(128)} %constant.74.clone.1), dimensions={0}, to_apply=%region_0.1 | reduce | flops 8126464 | bytes 34603012 | tf_op jit(solution)/shard_map/reduce_sum | solution.py:61
  267.4 11.7 %cholesky.214 = f32[128,128]{1,0:T(8,128)S(1)} custom-call(f32[128,128]{1,0:T(8,128)S(1)} %cholesky.346), custom_call_target="Cholesky" | custom-call | tf_op jit(solution)/shard_map/jit(cholesky)/cholesky | solution.py:19
  302.5 11.7 %cholesky.265 = f32[128,128]{1,0:T(8,128)S(1)} custom-call(f32[128,128]{1,0:T(8,128)S(1)} %convolution_subtract_fusion.8), custom_call_target="Cholesky" | custom-call | tf_op jit(solution)/shard_map/jit(cholesky)/cholesky | solution.py:19
  317.1 11.7 %cholesky.231 = f32[128,128]{1,0:T(8,128)S(1)} custom-call(f32[128,128]{1,0:T(8,128)S(1)} %convolution_subtract_fusion.9), custom_call_target="Cholesky" | custom-call | tf_op jit(solution)/shard_map/jit(cholesky)/cholesky | solution.py:19
  341.4 19.7 %custom-call.20 = f32[2,128,128]{1,2,0:T(8,128)S(1)} custom-call(f32[2,128,128]{2,1,0:T(8,128)S(1)} %get-tuple-element.39), custom_call_target="InvertDiagBlocksLowerTriangular" | custom-call | tf_op jit(solution)/shard_map/jit(_solve_triangular)/triangular_solve | solution.py:21
  361.1 19.7 %custom-call.18 = f32[2,128,128]{1,2,0:T(8,128)S(1)} custom-call(f32[2,128,128]{2,1,0:T(8,128)S(1)} %get-tuple-element.38), custom_call_target="InvertDiagBlocksLowerTriangular" | custom-call | tf_op jit(solution)/shard_map/jit(_solve_triangular)/triangular_solve | solution.py:21
  387.9 16.8 %all-reduce.11.cloned.1.call-done = f32[256,1536]{1,0:T(8,128)} async-done(((f32[256,1536]{1,0:T(8,128)}), f32[256,1536]{1,0:T(8,128)}) %all-reduce.11.cloned.1.call-update) | async-done | bytes 1572880 | tf_op jit(solution)/shard_map/psum | solution.py:11
  404.7 17.5 %fusion = f32[256,1536]{1,0:T(8,128)} fusion(f32[3072,256]{1,0:T(8,128)S(1)} %convolution_add_fusion, f32[1,3072,1,1536]{3,2,1,0:T(1,128)} %param.6), kind=kOutput, calls=%fused_computation.9 | convolution fusion | flops 7247757312 | bytes 23592960 | tf_op jit(solution)/shard_map/dot_general | solution.py:32
  422.1 17.3 %fusion.80 = f32[256,1536]{1,0:T(8,128)} fusion(f32[3072,256]{1,0:T(8,128)S(1)} %convolution_add_fusion, f32[1,3072,1,1536]{3,2,1,0:T(1,128)} %param.5), kind=kOutput, calls=%fused_computation.172 | convolution fusion | flops 7247757312 | bytes 23592960 | tf_op jit(solution)/shard_map/dot_general | solution.py:32
  444.7 15.4 %fusion.9 = f32[3072,256]{0,1:T(8,128)S(1)} fusion(f32[256,1536]{1,0:T(8,128)S(1)} %convolution_add_fusion.1, f32[1,3072,1,1536]{3,2,1,0:T(1,128)} %param.6), kind=kOutput, calls=%fused_computation.23 | convolution fusion | flops 7247757312 | bytes 23592960 | tf_op jit(solution)/shard_map/dot_general | solution.py:32
  460.1 15.3 %convolution_bitcast_fusion = f32[3072,256]{0,1:T(8,128)S(1)} fusion(f32[256,1536]{1,0:T(8,128)S(1)} %convolution_add_fusion.1, f32[1,3072,1,1536]{3,2,1,0:T(1,128)} %param.5), kind=kOutput, calls=%fused_computation.24 | convolution fusion | flops 7247757312 | bytes 23592960 | tf_op jit(solution)/shard_map/dot_general | solution.py:32
  509.8 13.2 %cholesky.299 = f32[128,128]{1,0:T(8,128)} custom-call(f32[128,128]{1,0:T(8,128)} %convolution_subtract_fusion.7), custom_call_target="Cholesky" | custom-call | tf_op jit(solution)/shard_map/jit(cholesky)/cholesky | solution.py:25
  533.6 21.1 %custom-call.22 = f32[2,128,128]{1,2,0:T(8,128)} custom-call(f32[2,128,128]{2,1,0:T(8,128)} %get-tuple-element.40), custom_call_target="InvertDiagBlocksLowerTriangular" | custom-call | tf_op jit(solution)/shard_map/jit(_solve_triangular)/triangular_solve | solution.py:27
  565.4 58.9 %reduce-scatter.2.cloned.1.call-done = f32[384,512]{0,1:T(8,128)} async-done(((f32[3072,512]{0,1:T(8,128)}), f32[384,512]{0,1:T(8,128)}) %reduce-scatter.2.cloned.1.call-update) | async-done | bytes 786448 | tf_op jit(solution)/shard_map/reduce_scatter | solution.py:75
  630.9 11.7 %cholesky.316 = f32[128,128]{1,0:T(8,128)S(1)} custom-call(f32[128,128]{1,0:T(8,128)S(1)} %cholesky.355), custom_call_target="Cholesky" | custom-call | tf_op jit(solution)/shard_map/jit(cholesky)/cholesky | solution.py:25
  653.0 12.1 %cholesky.333 = f32[128,128]{1,0:T(8,128)S(1)} custom-call(f32[128,128]{1,0:T(8,128)S(1)} %convolution_subtract_fusion.6), custom_call_target="Cholesky" | custom-call | tf_op jit(solution)/shard_map/jit(cholesky)/cholesky | solution.py:25
  671.7 19.7 %custom-call.24 = f32[2,128,128]{1,2,0:T(8,128)S(1)} custom-call(f32[2,128,128]{2,1,0:T(8,128)S(1)} %get-tuple-element.41), custom_call_target="InvertDiagBlocksLowerTriangular" | custom-call | tf_op jit(solution)/shard_map/jit(_solve_triangular)/triangular_solve | solution.py:27
  704.8 25.2 %all-gather.4.cloned.1.call-done = f32[3072,512]{1,0:T(8,128)} async-done(((f32[384,512]{1,0:T(8,128)}), f32[3072,512]{1,0:T(8,128)}) %all-gather.4.cloned.1.call-update) | async-done | bytes 6291472 | tf_op jit(solution)/shard_map/all_gather | solution.py:86
  735.2 23.6 %fusion.4 = f32[1,3072,1,1536]{3,1,2,0:T(8,128)} fusion(f32[1,3072,1,1536]{3,2,1,0:T(1,128)} %param.6, f32[3072,256]{1,0:T(8,128)S(1)} %copy-done.1, f32[3072,256]{1,0:T(8,128)} %get-tuple-element.88, f32[256,1536]{1,0:T(8,128)S(1)} %convolution_add_fusion.1, f32[256,1536]{1,0:T(8,128)S(1)} %copy-done.6), kind=kOutput, calls=%fused_computation.13 | convolution fusion | flops 14502592512 | bytes 47185920 | tf_op jit(solution)/shard_map/dot_general | solution.py:32
  758.8 22.3 %copy.23 = f32[1,3072,1,1536]{3,2,1,0:T(1,128)} copy(f32[1,3072,1,1536]{3,1,2,0:T(8,128)} %fusion.4) | data formatting | bytes 37748736
  781.0 22.8 %subtract_bitcast_fusion = f32[1,3072,1,1536]{3,1,2,0:T(8,128)} fusion(f32[3072,256]{1,0:T(8,128)S(1)} %copy-done.1, f32[3072,256]{1,0:T(8,128)S(1)} %get-tuple-element.89, f32[256,1536]{1,0:T(8,128)S(1)} %convolution_add_fusion.1, f32[256,1536]{1,0:T(8,128)S(1)} %fusion.92, f32[1,3072,1,1536]{3,2,1,0:T(1,128)} %param.5), kind=kOutput, calls=%fused_computation.15 | convolution fusion | flops 14502592512 | bytes 47185920 | tf_op jit(solution)/shard_map/dot_general | solution.py:32
  803.8 22.3 %copy.22 = f32[1,3072,1,1536]{3,2,1,0:T(1,128)} copy(f32[1,3072,1,1536]{3,1,2,0:T(8,128)} %subtract_bitcast_fusion) | data formatting | bytes 37748736
  (182 shorter events, 196.2 us)
Async XLA Ops:
  7.2 227.7 %all-gather.6.cloned.1.call-start = ((), (), s32[]{:S(2)}) async-start(), calls=%async_computation.6 | async-start | bytes 34603008 | tf_op jit(solution)/shard_map/all_gather | solution.py:61
  9.8 25.9 %copy-start.2 = (f32[1,256,1,1536]{3,1,2,0:T(8,128)}, f32[1,256,1,1536]{3,1,2,0:T(8,128)S(1)}, u32[]{:S(2)}) copy-start(f32[1,256,1,1536]{3,1,2,0:T(8,128)S(1)} %copy.48) | copy-start | bytes 4718596
  37.9 345.5 %all-reduce.9.cloned.1.call-start = ((), (), s32[]{:S(2)}) async-start(), calls=%async_computation.1 | async-start | bytes 6291456 | tf_op jit(solution)/shard_map/psum | solution.py:11
  249.7 1.2 copy-start.4
  249.7 155.0 %all-reduce.11.cloned.1.call-start = ((), (), s32[]{:S(2)}) async-start(), calls=%async_computation.2 | async-start | bytes 3145728 | tf_op jit(solution)/shard_map/psum | solution.py:11
  252.0 79.9 %copy-start.3 = (f32[1,256,1,1536]{3,1,2,0:T(8,128)S(1)}, f32[1,256,1,1536]{3,1,2,0:T(8,128)}, u32[]{:S(2)}) copy-start(f32[1,256,1,1536]{3,1,2,0:T(8,128)} %copy-done.2) | copy-start | bytes 4718596
  254.1 0.7 copy-start.13
  337.1 46.3 %copy-start.10 = (f32[256,256]{1,0:T(8,128)}, f32[256,256]{1,0:T(8,128)S(1)}, u32[]{:S(2)}) copy-start(f32[256,256]{1,0:T(8,128)S(1)} %get-tuple-element.327) | copy-start | bytes 786436
  337.1 222.8 %all-reduce.15.cloned.1.call-start = ((), (), s32[]{:S(2)}) async-start(), calls=%async_computation.7 | async-start | bytes 6291456 | tf_op jit(solution)/shard_map/psum | solution.py:72
  361.1 20.7 %copy-start.15 = (f32[2,128,128]{1,2,0:T(8,128)}, f32[2,128,128]{1,2,0:T(8,128)S(1)}, u32[]{:S(2)}) copy-start(f32[2,128,128]{1,2,0:T(8,128)S(1)} %custom-call.20) | copy-start | bytes 393220
  387.9 34.2 %copy-start = (f32[3072,256]{1,0:T(8,128)}, f32[3072,256]{1,0:T(8,128)S(1)}, u32[]{:S(2)}) copy-start(f32[3072,256]{1,0:T(8,128)S(1)} %convolution_add_fusion) | copy-start | bytes 9437188
  439.4 0.9 copy-start.9
  439.4 2.0 copy-start.16
  439.5 184.9 %reduce-scatter.2.cloned.1.call-start = ((), (), s32[]{:S(2)}) async-start(), calls=%async_computation.3 | async-start | bytes 7077888 | tf_op jit(solution)/shard_map/reduce_scatter | solution.py:75
  478.5 1.3 copy-start.5
  478.5 214.9 %all-reduce.13.cloned.1.call-start = ((), (), s32[]{:S(2)}) async-start(), calls=%async_computation.5 | async-start | bytes 1048576 | tf_op jit(solution)/shard_map/psum | solution.py:87
  482.6 0.7 copy-start.12
  495.0 0.6 copy-start.14
  524.5 2.0 copy-start.11
  559.8 3.0 copy-start.8
  565.2 164.9 %all-gather.4.cloned.1.call-start = ((), (), s32[]{:S(2)}) async-start(), calls=%async_computation.4 | async-start | bytes 7077888 | tf_op jit(solution)/shard_map/all_gather | solution.py:86
  696.2 5.7 copy-start.7
  730.1 5.1 copy-start.1
  730.1 5.1 copy-start.6
Sparse Core Ops, SparseCore 0:
  38.0 196.8 all-gather.5
  249.8 67.8 all-reduce.8
  337.2 67.4 all-reduce.10
  439.6 120.2 all-reduce.14
  563.6 60.6 reduce-scatter.1
  627.3 55.6 all-reduce.12
  685.5 44.5 all-gather.3
